TPU v7x, 32 devices: a whole 2x2x4 slice. The times are simulated.
32 devices in a mesh: dp: 4 (over z), expert: 4 (over y, core), tensor: 2 (over x).
Axes of the slice: x: 2, y: 2, z: 4, core: 2. Of those that a mesh axis runs over, the one named last changes fastest.
Arguments:
- hidden: bfloat16 [2048, 6144], P(('dp', 'expert'), 'tensor'), may hold values from -6 to 6
- expert_ids: int32 [2048, 8], P(('dp', 'expert')), may hold values from 0 to 383, as said below
- gate_fixed: int32 [2048, 8], P(('dp', 'expert')), may hold values from 4096 to 65535
- slot_expert: int32 [16], replicated, may hold values from 0 to 383, as said below
- expert_in: bfloat16 [16, 6144, 2, 1024], P(('dp', 'expert'), 'tensor'), may hold values from -1 to 1, as said below
- expert_out: bfloat16 [16, 1024, 6144], P(('dp', 'expert'), None, 'tensor'), may hold values from -1 to 1, as said below
- shared_in: bfloat16 [6144, 2, 1024], P('tensor', None, 'dp'), may hold values from -0.078125 to 0.078125
- shared_out: bfloat16 [1024, 6144], P('dp', 'tensor'), may hold values from -0.1875 to 0.1875
Outputs:
- mixed: bfloat16 [2048, 6144], P(('dp', 'expert'), 'tensor')
Inputs may be any that keep to these rules, and one draw needn't show every extreme that they name: `expert_ids`: each row names 8 different experts. `slot_expert`: 14 different experts fill the 16 slots; 2 of them hold two slots each, the others one. `expert_in`: slots that hold the same expert hold the same weights. `expert_out`: slots that hold the same expert hold the same weights.
All inputs are finite; a program needn't handle non-finite values.
Results may differ from a plain program's by a relative error of at most 0.006.
Values may be sent and summed in bfloat16 or wider, within the bound.
A program may use at most 192 MiB of HBM per device.

v0:
```python
import functools

import jax
import jax.numpy as jnp
from jax import lax
from jax.experimental import pallas as pl
from jax.experimental.pallas import tpu as pltpu
from jax.sharding import PartitionSpec as P

CAP = 4
BLOCK = 2 * CAP
LANES = 128
TILE = 256
RING = 4
gate_scale = 1.0 / 65536.0
BF = jnp.bfloat16
F32 = jnp.float32
MESH = pl.DeviceIdType.MESH


def dot(a, b):
    return jnp.dot(a, b, preferred_element_type=F32)


def silu(v):
    return v / (1.0 + jnp.exp(-v))


def slot_plan(expert_ids, gate_fixed, slot_expert):
    tok_rows, topk_count = expert_ids.shape
    slot_count = slot_expert.shape[0]
    slot_iota = jnp.arange(slot_count, dtype=jnp.int32)
    same = slot_expert[:, None] == slot_expert[None, :]
    copy_of = jnp.sum((same & (slot_iota[None, :] < slot_iota[:, None])).astype(jnp.int32), axis=1)
    place = jnp.arange(BLOCK, dtype=jnp.int32) % CAP
    first_rank = (copy_of[:, None] * CAP + place[None, :]).reshape(-1)
    usable = jnp.repeat(copy_of < 2, BLOCK)
    column_expert = jnp.repeat(slot_expert, BLOCK)
    named = jnp.zeros((tok_rows, slot_count * BLOCK), jnp.bool_)
    gate = jnp.zeros((tok_rows, slot_count * BLOCK), jnp.int32)
    for k in range(topk_count):
        hit = expert_ids[:, k : k + 1] == column_expert[None, :]
        named = named | hit
        gate = jnp.where(hit, gate_fixed[:, k : k + 1], gate)
    token_iota = jnp.arange(tok_rows, dtype=jnp.int32)
    earlier = (token_iota[:, None] > token_iota[None, :]).astype(BF)
    before = jnp.dot(earlier, named.astype(BF), preferred_element_type=F32).astype(jnp.int32)
    served = named & usable[None, :] & (before == first_rank[None, :])
    gate = jnp.where(served, gate, 0)
    high = (gate // 256).astype(F32) * (256.0 * gate_scale)
    low = (gate % 256).astype(F32) * gate_scale
    return served.astype(BF), high.astype(BF), low.astype(BF)


def rows_of_words(weight):
    depth, _, units = weight.shape
    return weight.reshape(depth, 2, units // LANES, LANES).transpose(0, 2, 1, 3).reshape(-1, LANES)


def sorter(units):
    groups = units // LANES
    depth = TILE // (2 * groups)
    out = lax.broadcasted_iota(jnp.int32, (TILE, TILE), 0)
    inner = lax.broadcasted_iota(jnp.int32, (TILE, TILE), 1)
    shift = (2 * groups).bit_length() - 1
    d = lax.shift_right_logical(inner, jnp.int32(shift))
    j = lax.shift_right_logical(inner & (2 * groups - 1), jnp.int32(1))
    g = inner & 1
    return ((g * groups + j) * depth + d == out).astype(F32).astype(BF)


def kernel(
    sizes, served_ref, high_ref, low_ref, hid_ref, ae_ref, we_ref, as_ref, ws_ref, out_ref,
    hid2, send, arr, ans, ret, ring, wp_e, wo_e, raw_s, wp_s, wo_s,
    pm_own, pm_send, pm_recv, act_e, sp_own, sp_send, sp_recv, acts, act_send, acc,
    s_sem, r_sem, out_s, out_r, back_s, back_r, l_sem, ring_sem,
):
    E = sizes
    tok, D = hid_ref.shape
    D2 = D // 2
    R = served_ref.shape[1]
    N = R // BLOCK
    F = we_ref.shape[0]
    S = ws_ref.shape[0]
    z, e, t = lax.axis_index("dp"), lax.axis_index("expert"), lax.axis_index("tensor")
    me = z * E + e
    z1 = z + 1 - 2 * (z % 2)
    z2 = z + 2 - 4 * (z // 2)
    quarter = e % 4
    yy = (e // 2) % 2
    e_y = e + 2 - 4 * yy
    e_c = e + 1 - 2 * (e % 2)
    q_y = quarter + 2 - 4 * yy
    near = (z1, e, t)
    far = (z2, e, t)
    side = (z, e_y, t)
    twin = (z, e_c, t)
    other = (z, e, 1 - t)

    def load(index, src, dst):
        copy = pltpu.make_async_copy(src, dst, l_sem.at[index])
        copy.start()
        return copy

    load_hid = load(0, hid_ref, hid2.at[pl.ds(0, tok)])
    chunk = ring.shape[1]
    chunks = ae_ref.shape[0] // chunk

    def ring_copy(index):
        slot = index % RING
        return pltpu.make_async_copy(
            ae_ref.at[pl.ds(pl.multiple_of(index * chunk, chunk), chunk)], ring.at[slot], ring_sem.at[slot]
        )

    for index in range(min(RING, chunks)):
        ring_copy(index).start()
    load_raw = load(1, as_ref, raw_s.at[0])
    load_wo_e = load(2, we_ref, wo_e)
    load_wo_s = load(3, ws_ref, wo_s.at[0])

    def place_of(offset):
        slot = (me + offset) % N
        return slot, (slot // E, slot % E, t)

    barrier = pltpu.get_barrier_semaphore()

    @pl.loop(1, N)
    def _(offset):
        pl.semaphore_signal(barrier, inc=1, device_id=place_of(offset)[1], device_id_type=MESH)

    pl.semaphore_signal(barrier, inc=1, device_id=other, device_id_type=MESH)

    column = lax.broadcasted_iota(jnp.int32, (tok, R), 1)
    first_half = (column & CAP) == 0

    def halves(ref):
        value = ref[...].astype(F32)
        return jnp.where(first_half, value, 0.0).astype(BF), jnp.where(first_half, 0.0, value).astype(BF)

    load_hid.wait()
    pick = halves(served_ref)
    across = (((0,), (0,)), ((), ()))

    @pl.loop(0, D2 // TILE)
    def _(n):
        c = pl.multiple_of(n * TILE, TILE)
        c2 = pl.multiple_of(n * TILE + D2, TILE)
        rows = lax.dot_general(pick[0], hid2[pl.ds(0, tok), pl.ds(c, TILE)], across, preferred_element_type=F32)
        rows += lax.dot_general(pick[1], hid2[pl.ds(0, tok), pl.ds(c2, TILE)], across, preferred_element_type=F32)
        send[:, pl.ds(c, TILE)] = rows.astype(BF)

    pl.semaphore_wait(barrier, N)

    count = [0]

    def remote(src, dst, device):
        index = count[0]
        count[0] += 1
        return pltpu.make_async_remote_copy(
            src_ref=src, dst_ref=dst, send_sem=s_sem.at[index], recv_sem=r_sem.at[index],
            device_id=device, device_id_type=MESH,
        )

    def block_copy(src, dst, sends, recvs, offset):
        slot, device = place_of(offset)
        return pltpu.make_async_remote_copy(
            src_ref=src.at[pl.ds(pl.multiple_of(slot * BLOCK, BLOCK), BLOCK)],
            dst_ref=dst.at[pl.ds(pl.multiple_of(me * BLOCK, BLOCK), BLOCK)],
            send_sem=sends.at[offset], recv_sem=recvs.at[offset],
            device_id=device, device_id_type=MESH,
        )

    @pl.loop(1, N)
    def _(offset):
        block_copy(send, arr, out_s, out_r, offset).start()

    started = []

    def go(copy):
        copy.start()
        started.append(copy)
        return copy

    tokens = go(remote(hid_ref, hid2.at[pl.ds(tok, tok)], near))

    parts = 2
    q_rows = as_ref.shape[0] // 4
    p_rows = q_rows // parts
    o_rows = S // 4

    def in_rows(q, p):
        return pl.ds(pl.multiple_of(q * q_rows + p * p_rows, p_rows), p_rows)

    def out_rows(q):
        return pl.ds(pl.multiple_of(q * o_rows, o_rows), o_rows)

    w_in = [go(remote(as_ref.at[in_rows(quarter, p)], raw_s.at[1, in_rows(quarter, p)], far)) for p in range(parts)]
    w_out = [None] * 4
    w_out[1] = go(remote(ws_ref.at[out_rows(quarter)], wo_s.at[1, out_rows(quarter)], far))
    w_out[2] = go(remote(ws_ref.at[out_rows(quarter)], wo_s.at[2, out_rows(quarter)], near))

    def sort_rows(source, one_hot, units, row, store):
        groups = units // LANES
        depth = TILE // (2 * groups)
        pair = jnp.concatenate([source(row), source(row + TILE)], axis=1)
        mixed = dot(one_hot, pair).astype(BF)
        for g in range(2):
            for j in range(groups):
                at = (g * groups + j) * depth
                for half in range(2):
                    store(g, half * depth, depth, j, mixed[at : at + depth, half * LANES : (half + 1) * LANES])

    one_hot_e = sorter(F)
    depth_e = chunk // (2 * (F // LANES))

    @pl.loop(0, chunks)
    def _(index):
        slot = index % RING
        ring_copy(index).wait()

        @pl.loop(0, chunk // (2 * TILE))
        def _(pair):
            base = pl.multiple_of(index * depth_e + pair * (2 * TILE // (2 * (F // LANES))), 16)

            def store(g, first, depth, j, block):
                wp_e[g, pl.ds(pl.multiple_of(base + first, 16), depth), pl.ds(j * LANES, LANES)] = block

            def source(row):
                return ring[slot, pl.ds(pl.multiple_of(row, TILE), TILE), :]

            sort_rows(source, one_hot_e, F, pair * (2 * TILE), store)

        @pl.when(index + RING < chunks)
        def _():
            ring_copy(index + RING).start()

    def sort_shared(k):
        one_hot = sorter(S)
        step = 2 * TILE // (2 * (S // LANES))

        @pl.loop(0, as_ref.shape[0] // (2 * TILE))
        def _(pair):
            base = pl.multiple_of(pair * step, step)

            def store(g, first, depth, j, block):
                wp_s[k, g, pl.ds(pl.multiple_of(base + first, 16), depth), pl.ds(j * LANES, LANES)] = block

            def source(row):
                return raw_s[k, pl.ds(pl.multiple_of(row, TILE), TILE), :]

            sort_rows(source, one_hot, S, pair * (2 * TILE), store)

    load_raw.wait()
    sort_shared(0)

    row_of = lax.broadcasted_iota(jnp.int32, (R, TILE), 0)
    upper = (row_of & CAP) == 0
    mine = lax.shift_right_logical(row_of, jnp.int32(BLOCK.bit_length() - 1)) == me

    def own_block(whole, own):
        @pl.loop(0, D2 // TILE)
        def _(n):
            c = pl.ds(pl.multiple_of(n * TILE, TILE), TILE)
            whole[:, c] = jnp.where(mine, own[:, c].astype(F32), whole[:, c].astype(F32)).astype(BF)

    @pl.loop(1, N)
    def _(offset):
        block_copy(send, arr, out_s, out_r, offset).wait_recv()

    own_block(arr, send)

    mid = [remote(pm_send.at[n], pm_recv.at[n], other) for n in range(F // TILE)]
    for n in range(F // TILE):
        c = pl.ds(n * TILE, TILE)
        gate = dot(arr[...], wp_e[0, :D2, c]) + pltpu.roll(dot(arr[...], wp_e[0, D2:, c]), R - CAP, 0)
        up = pltpu.roll(dot(arr[...], wp_e[1, :D2, c]), CAP, 0) + dot(arr[...], wp_e[1, D2:, c])
        both = jnp.where(upper, gate, up)
        pm_own[n] = both
        pm_send[n] = both.astype(BF)
        go(mid[n])

    shared_mid = [remote(sp_send.at[k], sp_recv.at[k], other) for k in range(2)]
    act_back = [remote(act_send.at[k], acts.at[2 + k], near) for k in range(2)]

    def shared_up(k):
        for g in range(2):
            part = dot(hid2[...], wp_s[k, g])
            sp_own[k, g] = part
            sp_send[k, g] = part.astype(BF)
        go(shared_mid[k])

    def shared_act(k):
        shared_mid[k].wait_recv()
        gate = sp_own[k, 0] + sp_recv[k, 0].astype(F32)
        up = sp_own[k, 1] + sp_recv[k, 1].astype(F32)
        act = (silu(gate) * up).astype(BF)
        acts[k] = act[:tok]
        act_send[k] = act[tok:]
        go(act_back[k])

    tokens.wait_recv()
    shared_up(0)

    in_side = [remote(raw_s.at[1, in_rows(quarter, p)], raw_s.at[1, in_rows(quarter, p)], side) for p in range(parts)]
    in_twin = [remote(raw_s.at[1, in_rows(quarter, p)], raw_s.at[1, in_rows(quarter, p)], twin) for p in range(parts)]
    in_twin2 = [remote(raw_s.at[1, in_rows(q_y, p)], raw_s.at[1, in_rows(q_y, p)], twin) for p in range(parts)]
    out_side, out_twin, out_twin2 = {}, {}, {}
    for k in (1, 2, 3):
        rows, rows_y = wo_s.at[k, out_rows(quarter)], wo_s.at[k, out_rows(q_y)]
        out_side[k], out_twin[k], out_twin2[k] = remote(rows, rows, side), remote(rows, rows, twin), remote(rows_y, rows_y, twin)
    w_out[3] = remote(wo_s.at[1, out_rows(quarter)], wo_s.at[3, out_rows(quarter)], near)

    def spread_in(p):
        w_in[p].wait_recv()
        go(in_side[p])
        go(in_twin[p])

    def spread_out(k):
        w_out[k].wait_recv()
        go(out_side[k])
        go(out_twin[k])

    def pass_out(k):
        out_side[k].wait_recv()
        go(out_twin2[k])

    def have_out(k):
        out_twin[k].wait_recv()
        out_twin2[k].wait_recv()

    spread_in(0)

    load_wo_e.wait()
    for n in range(F // TILE):
        mid[n].wait_recv()
        total = pm_own[n] + pm_recv[n].astype(F32)
        act = silu(total) * pltpu.roll(total, R - CAP, 0)
        act_e[:, pl.ds(n * TILE, TILE)] = act.astype(BF)

    @pl.loop(0, D2 // TILE)
    def _(n):
        c = pl.multiple_of(n * TILE, TILE)
        c2 = pl.multiple_of(n * TILE + D2, TILE)
        one = dot(act_e[...], wo_e[:, pl.ds(c, TILE)])
        two = dot(act_e[...], wo_e[:, pl.ds(c2, TILE)])
        ans[:, pl.ds(c, TILE)] = jnp.where(upper, one, pltpu.roll(two, CAP, 0)).astype(BF)

    @pl.loop(1, N)
    def _(offset):
        block_copy(ans, ret, back_s, back_r, offset).start()

    spread_in(1)
    for p in range(2, parts):
        spread_in(p)
    shared_act(0)
    for p in range(parts):
        in_side[p].wait_recv()
        go(in_twin2[p])
    w_out[1].wait_recv()
    go(w_out[3])
    go(out_side[1])
    go(out_twin[1])
    spread_out(2)

    for p in range(parts):
        in_twin[p].wait_recv()
        in_twin2[p].wait_recv()
    sort_shared(1)
    shared_up(1)
    pass_out(1)
    pass_out(2)
    load_wo_s.wait()
    shared_act(1)
    have_out(1)

    @pl.loop(0, D // TILE)
    def _(n):
        c = pl.ds(pl.multiple_of(n * TILE, TILE), TILE)
        acc[:, c] = dot(acts[0], wo_s[0, :, c]) + dot(acts[1], wo_s[1, :, c])

    spread_out(3)

    @pl.loop(1, N)
    def _(offset):
        block_copy(ans, ret, back_s, back_r, offset).wait_recv()

    own_block(ret, ans)
    high, low = halves(high_ref), halves(low_ref)
    have_out(2)
    act_back[0].wait_recv()
    for half in range(2):
        @pl.loop(0, D2 // TILE)
        def _(n):
            c = pl.ds(pl.multiple_of(n * TILE + half * D2, TILE), TILE)
            back = ret[:, pl.ds(pl.multiple_of(n * TILE, TILE), TILE)]
            acc[:, c] += dot(acts[2], wo_s[2, :, c]) + dot(high[half], back) + dot(low[half], back)

    pass_out(3)
    act_back[1].wait_recv()
    have_out(3)

    @pl.loop(0, D // TILE)
    def _(n):
        c = pl.ds(pl.multiple_of(n * TILE, TILE), TILE)
        out_ref[:, c] = (acc[:, c] + dot(acts[3], wo_s[3, :, c])).astype(BF)

    @pl.loop(1, N)
    def _(offset):
        block_copy(send, arr, out_s, out_r, offset).wait_send()
        block_copy(ans, ret, back_s, back_r, offset).wait_send()

    for copy in started:
        copy.wait_send()


def solution(mesh):
    expert_size = mesh.shape["expert"]

    def shards(
        hidden, expert_ids, gate_fixed, slot_expert, expert_in, expert_out, shared_in, shared_out
    ):
        tok, D = hidden.shape
        F = expert_out.shape[1]
        S = shared_out.shape[0]
        N = slot_expert.shape[0]
        R = N * BLOCK
        served, high, low = slot_plan(expert_ids, gate_fixed, slot_expert)
        a_e = rows_of_words(expert_in[0])
        a_s = rows_of_words(shared_in)
        chunk = a_e.shape[0] // 16
        vmem = pl.BlockSpec(memory_space=pltpu.VMEM)
        hbm = pl.BlockSpec(memory_space=pl.ANY)
        dma = pltpu.SemaphoreType.DMA
        return pl.pallas_call(
            functools.partial(kernel, expert_size),
            out_shape=jax.ShapeDtypeStruct((tok, D), BF),
            in_specs=[vmem] * 3 + [hbm] * 5,
            out_specs=vmem,
            scratch_shapes=[
                pltpu.VMEM((2 * tok, D), BF),
                pltpu.VMEM((R, D // 2), BF),
                pltpu.VMEM((R, D // 2), BF),
                pltpu.VMEM((R, D // 2), BF),
                pltpu.VMEM((R, D // 2), BF),
                pltpu.VMEM((RING, chunk, LANES), BF),
                pltpu.VMEM((2, D, F), BF),
                pltpu.VMEM((F, D), BF),
                pltpu.VMEM((2, a_s.shape[0], LANES), BF),
                pltpu.VMEM((2, 2, D, S), BF),
                pltpu.VMEM((4, S, D), BF),
                pltpu.VMEM((F // TILE, R, TILE), F32),
                pltpu.VMEM((F // TILE, R, TILE), BF),
                pltpu.VMEM((F // TILE, R, TILE), BF),
                pltpu.VMEM((R, F), BF),
                pltpu.VMEM((2, 2, 2 * tok, S), F32),
                pltpu.VMEM((2, 2, 2 * tok, S), BF),
                pltpu.VMEM((2, 2, 2 * tok, S), BF),
                pltpu.VMEM((4, tok, S), BF),
                pltpu.VMEM((2, tok, S), BF),
                pltpu.VMEM((tok, D), F32),
                dma((64,)),
                dma((64,)),
                dma((N,)),
                dma((N,)),
                dma((N,)),
                dma((N,)),
                dma((4,)),
                dma((RING,)),
            ],
            compiler_params=pltpu.CompilerParams(
                collective_id=0, has_side_effects=True, vmem_limit_bytes=62 * 2**20
            ),
        )(served, high, low, hidden, a_e, expert_out[0], a_s, shared_out)

    in_specs = (
        P(("dp", "expert"), "tensor"),
        P(("dp", "expert"), None),
        P(("dp", "expert"), None),
        P(),
        P(("dp", "expert"), "tensor", None, None),
        P(("dp", "expert"), None, "tensor"),
        P("tensor", None, "dp"),
        P("dp", "tensor"),
    )
    out_specs = P(("dp", "expert"), "tensor")
    return jax.shard_map(
        shards, mesh=mesh, in_specs=in_specs, out_specs=out_specs, check_vma=False
    )
```

profile of v0, /device:TPU:1, one launch (start us, length us, event | category | flops | bytes accessed | tf_op | source)
XLA Modules:
  0.0 116.7 jit_solution(14818380774664933184)
XLA Ops:
  0.0 0.9 convert_reduce_fusion
  0.9 0.1 broadcast_in_dim.79
  1.0 0.1 and.39
  1.1 0.1 broadcast_add_fusion
  1.2 0.1 add.41
  1.3 0.7 broadcast_in_dim.78
  2.0 0.1 eq.67
  2.1 1.0 slice_bitcast_fusion.7
  3.1 1.0 fusion.22
  4.1 1.0 fusion.8
  5.0 0.7 fusion.5.high_ref
  5.7 108.9 %shard_map.82 = bf16[128,3072]{1,0:T(8,128)(2,1)} custom-call(bf16[128,128]{1,0:T(8,128)(2,1)} %get-tuple-element.23.served_ref, bf16[128,128]{1,0:T(8,128)(2,1)} %fusion.5.high_ref, bf16[128,128]{1,0:T(8,128)(2,1)} %get-tuple-element.5.low_ref, bf16[128,3072]{1,0:T(8,128)(2,1)} %hid_ref.1, bf16[49152,128]{1,0:T(8,128)(2,1)} %bitcast.43, ...), custom_call_target="tpu_custom_call" | custom-call | tf_op jit(solution)/shard_map/pallas_call | solution.py:434
  114.6 2.1 %copy.16 = bf16[128,3072]{1,0:T(8,128)(2,1)} copy(bf16[128,3072]{1,0:T(8,128)(2,1)} %shard_map.82) | data formatting | bytes 1572864
  (3 shorter events, 0.0 us)
where the time goes:
time: 117 us
  Pallas kernels  109 us (93%)
  local copies, waits for them, and re-layouts  4.14 us (4%)
  other arithmetic  2.61 us (2%)
    pallas_call x1, Pallas kernels, shards(): pl.pallas_call(functools.partial(kernel, expert_size), out_shape=jax.Shap...  109 us

commit v1 on v0

v1 whole, which is shorter than its diff:
```python
import functools

import jax
import jax.numpy as jnp
from jax import lax
from jax.experimental import pallas as pl
from jax.experimental.pallas import tpu as pltpu
from jax.sharding import PartitionSpec as P

CAP = 4
BLOCK = 2 * CAP
LANES = 128
TILE = 256
RING = 4
gate_scale = 1.0 / 65536.0
BF = jnp.bfloat16
F32 = jnp.float32
MESH = pl.DeviceIdType.MESH


def dot(a, b):
    return jnp.dot(a, b, preferred_element_type=F32)


def silu(v):
    return v / (1.0 + jnp.exp(-v))


def rows_of_words(weight):
    depth, _, units = weight.shape
    return weight.reshape(depth, 2, units // LANES, LANES).transpose(0, 2, 1, 3).reshape(-1, LANES)


def sorter(units):
    groups = units // LANES
    depth = TILE // (2 * groups)
    out = lax.broadcasted_iota(jnp.int32, (TILE, TILE), 0)
    inner = lax.broadcasted_iota(jnp.int32, (TILE, TILE), 1)
    shift = (2 * groups).bit_length() - 1
    d = lax.shift_right_logical(inner, jnp.int32(shift))
    j = lax.shift_right_logical(inner & (2 * groups - 1), jnp.int32(1))
    g = inner & 1
    return ((g * groups + j) * depth + d == out).astype(F32).astype(BF)


def kernel(
    E, ids_hbm, fixed_hbm, slot_hbm, hid_ref, ae_ref, we_ref, as_ref, ws_ref, out_ref,
    ids_ref, fixed_ref, slot_ref, hid2, pick, high, low, send, arr, ans, ret, ring, wp_e, wo_e, raw_s, wp_s, wo_s,
    pm_own, pm_send, pm_recv, act_e, sp_own, sp_send, sp_recv, acts, act_send, acc,
    s_sem, r_sem, out_s, out_r, back_s, back_r, l_sem, ring_sem,
):
    tok, D = hid_ref.shape
    D2 = D // 2
    N = slot_ref.shape[1]
    R = N * BLOCK
    F = we_ref.shape[0]
    S = ws_ref.shape[0]
    z, e, t = lax.axis_index("dp"), lax.axis_index("expert"), lax.axis_index("tensor")
    me = z * E + e
    z1 = z + 1 - 2 * (z % 2)
    z2 = z + 2 - 4 * (z // 2)
    quarter = e % 4
    yy = (e // 2) % 2
    e_y = e + 2 - 4 * yy
    e_c = e + 1 - 2 * (e % 2)
    q_y = quarter + 2 - 4 * yy
    near = (z1, e, t)
    far = (z2, e, t)
    side = (z, e_y, t)
    twin = (z, e_c, t)
    other = (z, e, 1 - t)

    def load(index, src, dst):
        copy = pltpu.make_async_copy(src, dst, l_sem.at[index])
        copy.start()
        return copy

    load_small = [load(4, ids_hbm, ids_ref), load(5, fixed_hbm, fixed_ref), load(6, slot_hbm, slot_ref)]
    load_hid = load(0, hid_ref, hid2.at[pl.ds(0, tok)])
    chunk = ring.shape[1]
    chunks = ae_ref.shape[0] // chunk

    def ring_copy(index):
        slot = index % RING
        return pltpu.make_async_copy(
            ae_ref.at[pl.ds(pl.multiple_of(index * chunk, chunk), chunk)], ring.at[slot], ring_sem.at[slot]
        )

    def place_of(offset):
        slot = (me + offset) % N
        return slot, (slot // E, slot % E, t)

    barrier = pltpu.get_barrier_semaphore()

    @pl.loop(1, N)
    def _(offset):
        pl.semaphore_signal(barrier, inc=1, device_id=place_of(offset)[1], device_id_type=MESH)

    pl.semaphore_signal(barrier, inc=1, device_id=other, device_id_type=MESH)

    for index in range(min(RING, chunks)):
        ring_copy(index).start()
    load_raw = load(1, as_ref, raw_s.at[0])
    load_wo_e = load(2, we_ref, wo_e)
    load_wo_s = load(3, ws_ref, wo_s.at[0])

    for small in load_small:
        small.wait()
    with jax.named_scope("plan"):
        slot_of = lax.shift_right_logical(
            lax.broadcasted_iota(jnp.int32, (R, N), 0), jnp.int32(BLOCK.bit_length() - 1)
        )
        lane = lax.broadcasted_iota(jnp.int32, (R, N), 1)
        held = jnp.broadcast_to(slot_ref[...].astype(F32), (R, N))
        expert = jnp.sum(jnp.where(lane == slot_of, held, 0.0), axis=1, keepdims=True)
        copy_of = jnp.sum(jnp.where((held == expert) & (lane < slot_of), 1.0, 0.0), axis=1, keepdims=True)
        row = lax.broadcasted_iota(jnp.int32, (R, tok), 0)
        first_rank = copy_of * CAP + (row & (CAP - 1)).astype(F32)
        named = jnp.zeros((R, tok), F32)
        gate = jnp.zeros((R, tok), jnp.int32)
        for k in range(ids_ref.shape[0]):
            hit = jnp.broadcast_to(ids_ref[k : k + 1, :].astype(F32), (R, tok)) == expert
            named = jnp.where(hit, 1.0, named)
            gate = jnp.where(hit, jnp.broadcast_to(fixed_ref[k : k + 1, :], (R, tok)), gate)
        early = lax.broadcasted_iota(jnp.int32, (tok, tok), 0) < lax.broadcasted_iota(jnp.int32, (tok, tok), 1)
        before = dot(named.astype(BF), jnp.where(early, 1.0, 0.0).astype(BF))
        served = (named > 0.0) & (copy_of < 2.0) & (before == first_rank)
        gate = jnp.where(served, gate, 0)
        top = (row & CAP) == 0
        high_all = lax.shift_right_logical(gate, jnp.int32(8)).astype(F32) * (256.0 * gate_scale)
        low_all = (gate & 255).astype(F32) * gate_scale
        for half in range(2):
            keep = top if half == 0 else jnp.logical_not(top)
            pick[half] = jnp.where(served & keep, 1.0, 0.0).astype(BF)
            high[half] = jnp.where(keep, high_all, 0.0).astype(BF)
            low[half] = jnp.where(keep, low_all, 0.0).astype(BF)

    with jax.named_scope("gather_rows"):
        load_hid.wait()

        @pl.loop(0, D2 // TILE)
        def _(n):
            c = pl.multiple_of(n * TILE, TILE)
            c2 = pl.multiple_of(n * TILE + D2, TILE)
            rows = dot(pick[0], hid2[pl.ds(0, tok), pl.ds(c, TILE)])
            rows += dot(pick[1], hid2[pl.ds(0, tok), pl.ds(c2, TILE)])
            send[:, pl.ds(c, TILE)] = rows.astype(BF)

    with jax.named_scope("barrier"):
        pl.semaphore_wait(barrier, N)

    count = [0]

    def remote(src, dst, device):
        index = count[0]
        count[0] += 1
        return pltpu.make_async_remote_copy(
            src_ref=src, dst_ref=dst, send_sem=s_sem.at[index], recv_sem=r_sem.at[index],
            device_id=device, device_id_type=MESH,
        )

    def block_copy(src, dst, sends, recvs, offset):
        slot, device = place_of(offset)
        return pltpu.make_async_remote_copy(
            src_ref=src.at[pl.ds(pl.multiple_of(slot * BLOCK, BLOCK), BLOCK)],
            dst_ref=dst.at[pl.ds(pl.multiple_of(me * BLOCK, BLOCK), BLOCK)],
            send_sem=sends.at[offset], recv_sem=recvs.at[offset],
            device_id=device, device_id_type=MESH,
        )

    @pl.loop(1, N)
    def _(offset):
        block_copy(send, arr, out_s, out_r, offset).start()

    started = []

    def go(copy):
        copy.start()
        started.append(copy)
        return copy

    q_rows = as_ref.shape[0] // 4
    parts = max(p for p in (1, 2, 3) if q_rows % (2 * TILE * p) == 0)
    p_rows = q_rows // parts
    o_parts = 2
    o_rows = S // (4 * o_parts)
    pieces = [(k, p) for k in (1, 2, 3) for p in range(o_parts)]

    def in_rows(q, p):
        return pl.ds(pl.multiple_of(q * q_rows + p * p_rows, p_rows), p_rows)

    def out_rows(q, p):
        return pl.ds(pl.multiple_of((q * o_parts + p) * o_rows, o_rows), o_rows)

    def in_place(q, p, device):
        return remote(raw_s.at[1, in_rows(q, p)], raw_s.at[1, in_rows(q, p)], device)

    def out_place(k, q, p, device):
        return remote(wo_s.at[k, out_rows(q, p)], wo_s.at[k, out_rows(q, p)], device)

    w_out = {}

    def send_out(k, device):
        for p in range(o_parts):
            rows = out_rows(quarter, p)
            w_out[k, p] = go(remote(ws_ref.at[rows], wo_s.at[k, rows], device))

    send_out(1, far)
    send_out(2, near)
    tokens = go(remote(hid_ref, hid2.at[pl.ds(tok, tok)], near))
    w_in = [go(remote(as_ref.at[in_rows(quarter, p)], raw_s.at[1, in_rows(quarter, p)], far)) for p in range(parts)]
    for p in range(o_parts):
        rows = out_rows(quarter, p)
        w_out[3, p] = remote(wo_s.at[1, rows], wo_s.at[3, rows], near)
    in_side = [in_place(quarter, p, side) for p in range(parts)]
    in_twin = [in_place(quarter, p, twin) for p in range(parts)]
    in_twin2 = [in_place(q_y, p, twin) for p in range(parts)]
    out_side = {(k, p): out_place(k, quarter, p, side) for k, p in pieces}
    out_twin = {(k, p): out_place(k, quarter, p, twin) for k, p in pieces}
    out_twin2 = {(k, p): out_place(k, q_y, p, twin) for k, p in pieces}
    mid = [remote(pm_send.at[n], pm_recv.at[n], other) for n in range(F // TILE)]
    shared_mid = {(k, h): remote(sp_send.at[k, h], sp_recv.at[k, h], other) for k in range(2) for h in range(2)}
    act_back = [remote(act_send.at[k], acts.at[2 + k], near) for k in range(2)]

    def sort_rows(source, one_hot, units, row, store):
        groups = units // LANES
        depth = TILE // (2 * groups)
        pair = jnp.concatenate([source(row), source(row + TILE)], axis=1)
        mixed = dot(one_hot, pair).astype(BF)
        for g in range(2):
            for j in range(groups):
                at = (g * groups + j) * depth
                for half in range(2):
                    store(g, half * depth, depth, j, mixed[at : at + depth, half * LANES : (half + 1) * LANES])

    def sort_expert():
        one_hot = sorter(F)
        per_pair = 2 * TILE // (2 * (F // LANES))
        per_chunk = chunk // (2 * (F // LANES))
        pairs = chunk // (2 * TILE)
        together = 2 if pairs % 2 == 0 else 1

        @pl.loop(0, chunks)
        def _(index):
            slot = index % RING
            ring_copy(index).wait()

            @pl.loop(0, pairs // together)
            def _(step):
                for u in range(together):
                    pair = step * together + u
                    base = pl.multiple_of(index * per_chunk + pair * per_pair, 16)

                    def store(g, first, depth, j, block):
                        wp_e[g, pl.ds(pl.multiple_of(base + first, 16), depth), pl.ds(j * LANES, LANES)] = block

                    def source(row):
                        return ring[slot, pl.ds(pl.multiple_of(row, TILE), TILE), :]

                    sort_rows(source, one_hot, F, pair * (2 * TILE), store)

            @pl.when(index + RING < chunks)
            def _():
                ring_copy(index + RING).start()

    def sort_shared(k, first_pair, pairs):
        one_hot = sorter(S)
        per_pair = 2 * TILE // (2 * (S // LANES))
        together = 2 if pairs % 2 == 0 else 1

        @pl.loop(0, pairs // together)
        def _(step):
            for u in range(together):
                pair = first_pair + step * together + u
                base = pl.multiple_of(pair * per_pair, per_pair)

                def store(g, first, depth, j, block):
                    wp_s[k, g, pl.ds(pl.multiple_of(base + first, 16), depth), pl.ds(j * LANES, LANES)] = block

                def source(row):
                    return raw_s[k, pl.ds(pl.multiple_of(row, TILE), TILE), :]

                sort_rows(source, one_hot, S, pair * (2 * TILE), store)

    row_of = lax.broadcasted_iota(jnp.int32, (R, TILE), 0)
    upper = (row_of & CAP) == 0
    mine = lax.shift_right_logical(row_of, jnp.int32(BLOCK.bit_length() - 1)) == me

    def own_block(whole, own):
        @pl.loop(0, D2 // TILE)
        def _(n):
            c = pl.ds(pl.multiple_of(n * TILE, TILE), TILE)
            whole[:, c] = jnp.where(mine, own[:, c].astype(F32), whole[:, c].astype(F32)).astype(BF)

    def routed_up():
        @pl.loop(1, N)
        def _(offset):
            block_copy(send, arr, out_s, out_r, offset).wait_recv()

        own_block(arr, send)
        for n in range(F // TILE):
            c = pl.ds(n * TILE, TILE)
            gate = dot(arr[...], wp_e[0, :D2, c]) + pltpu.roll(dot(arr[...], wp_e[0, D2:, c]), R - CAP, 0)
            up = pltpu.roll(dot(arr[...], wp_e[1, :D2, c]), CAP, 0) + dot(arr[...], wp_e[1, D2:, c])
            both = jnp.where(upper, gate, up)
            pm_own[n] = both
            pm_send[n] = both.astype(BF)
            go(mid[n])

    def routed_down():
        load_wo_e.wait()
        for n in range(F // TILE):
            mid[n].wait_recv()
            total = pm_own[n] + pm_recv[n].astype(F32)
            act = silu(total) * pltpu.roll(total, R - CAP, 0)
            act_e[:, pl.ds(n * TILE, TILE)] = act.astype(BF)

        @pl.loop(0, D2 // TILE)
        def _(n):
            c = pl.multiple_of(n * TILE, TILE)
            c2 = pl.multiple_of(n * TILE + D2, TILE)
            one = dot(act_e[...], wo_e[:, pl.ds(c, TILE)])
            two = dot(act_e[...], wo_e[:, pl.ds(c2, TILE)])
            ans[:, pl.ds(c, TILE)] = jnp.where(upper, one, pltpu.roll(two, CAP, 0)).astype(BF)

        @pl.loop(1, N)
        def _(offset):
            block_copy(ans, ret, back_s, back_r, offset).start()

    def shared_up(k, h):
        for g in range(2):
            part = dot(hid2[h * tok : (h + 1) * tok, :], wp_s[k, g])
            sp_own[k, h, g] = part
            sp_send[k, h, g] = part.astype(BF)
        go(shared_mid[k, h])

    def shared_act(k, h):
        shared_mid[k, h].wait_recv()
        gate = sp_own[k, h, 0] + sp_recv[k, h, 0].astype(F32)
        up = sp_own[k, h, 1] + sp_recv[k, h, 1].astype(F32)
        act = (silu(gate) * up).astype(BF)
        if h == 0:
            acts[k] = act
        else:
            act_send[k] = act
            go(act_back[k])

    def spread_in(p):
        w_in[p].wait_recv()
        go(in_side[p])
        go(in_twin[p])

    def pass_in(p):
        in_side[p].wait_recv()
        go(in_twin2[p])

    def sort_in(p):
        in_twin[p].wait_recv()
        in_twin2[p].wait_recv()
        for q in range(4):
            sort_shared(1, (q * q_rows + p * p_rows) // (2 * TILE), p_rows // (2 * TILE))

    def spread_out(k, p):
        w_out[k, p].wait_recv()
        if k == 1:
            go(w_out[3, p])
        go(out_side[k, p])
        go(out_twin[k, p])

    def pass_out(k, p):
        out_side[k, p].wait_recv()
        go(out_twin2[k, p])

    def have_out(k):
        for p in range(o_parts):
            out_twin[k, p].wait_recv()
            out_twin2[k, p].wait_recv()

    wide = 2 * TILE

    def wide_tiles(width, body):
        @pl.loop(0, width // wide)
        def _(n):
            body(pl.multiple_of(n * wide, wide))

    def scope(name, function, *args):
        with jax.named_scope(name):
            function(*args)

    last = parts - 1
    scope("sort_e", sort_expert)
    scope("routed_up", routed_up)
    load_raw.wait()
    scope("sort_s0", sort_shared, 0, 0, as_ref.shape[0] // (2 * TILE))
    scope("shared_up00", shared_up, 0, 0)
    for p in range(o_parts):
        scope(f"spread_out1{p}", spread_out, 1, p)
    scope("routed_down", routed_down)
    for p in range(o_parts):
        scope(f"spread_out2{p}", spread_out, 2, p)
    scope("shared_act00", shared_act, 0, 0)
    for k in (1, 2):
        for p in range(o_parts):
            scope(f"pass_out{k}{p}", pass_out, k, p)
    for p in range(last):
        scope(f"spread_in{p}", spread_in, p)
        if p > 0:
            scope(f"pass_in{p - 1}", pass_in, p - 1)
    scope("wait_tokens", tokens.wait_recv)
    scope("shared_up01", shared_up, 0, 1)
    scope(f"spread_in{last}", spread_in, last)
    if last > 0:
        scope(f"pass_in{last - 1}", pass_in, last - 1)
    for p in range(last):
        scope(f"sort_in{p}", sort_in, p)
    scope("shared_act01", shared_act, 0, 1)
    scope(f"pass_in{last}", pass_in, last)
    scope("spread_out30", spread_out, 3, 0)
    scope(f"sort_in{last}", sort_in, last)
    scope("shared_up11", shared_up, 1, 1)
    scope("shared_up10", shared_up, 1, 0)
    for p in range(1, o_parts):
        scope(f"spread_out3{p}", spread_out, 3, p)
    scope("shared_act11", shared_act, 1, 1)
    scope("pass_out30", pass_out, 3, 0)
    scope("shared_act10", shared_act, 1, 0)
    load_wo_s.wait()
    scope("have_out1", have_out, 1)

    def first_sum(c):
        acc[:, pl.ds(c, wide)] = dot(acts[0], wo_s[0, :, pl.ds(c, wide)]) + dot(acts[1], wo_s[1, :, pl.ds(c, wide)])

    scope("first_sum", wide_tiles, D, first_sum)
    scope("have_out2", have_out, 2)
    scope("act_back0", act_back[0].wait_recv)

    def second_sum(c):
        acc[:, pl.ds(c, wide)] += dot(acts[2], wo_s[2, :, pl.ds(c, wide)])

    scope("second_sum", wide_tiles, D, second_sum)
    for p in range(1, o_parts):
        scope(f"pass_out3{p}", pass_out, 3, p)

    def returned():
        @pl.loop(1, N)
        def _(offset):
            block_copy(ans, ret, back_s, back_r, offset).wait_recv()

        own_block(ret, ans)

    scope("returned", returned)
    scope("act_back1", act_back[1].wait_recv)
    scope("have_out3", have_out, 3)
    across = (((0,), (0,)), ((), ()))

    def third_sum(half):
        def body(c):
            back = ret[:, pl.ds(c, wide)]
            at = pl.ds(pl.multiple_of(c + half * D2, wide), wide)
            routed = lax.dot_general(high[half], back, across, preferred_element_type=F32)
            routed += lax.dot_general(low[half], back, across, preferred_element_type=F32)
            out_ref[:, at] = (acc[:, at] + routed + dot(acts[3], wo_s[3, :, at])).astype(BF)

        wide_tiles(D2, body)

    for half in range(2):
        scope(f"third_sum{half}", third_sum, half)

    @pl.loop(1, N)
    def _(offset):
        block_copy(send, arr, out_s, out_r, offset).wait_send()
        block_copy(ans, ret, back_s, back_r, offset).wait_send()

    for copy in started:
        copy.wait_send()


def solution(mesh):
    expert_size = mesh.shape["expert"]

    def shards(
        hidden, expert_ids, gate_fixed, slot_expert, expert_in, expert_out, shared_in, shared_out
    ):
        tok, D = hidden.shape
        F = expert_out.shape[1]
        S = shared_out.shape[0]
        N, topk = slot_expert.shape[0], expert_ids.shape[1]
        R = N * BLOCK
        a_e = rows_of_words(expert_in[0])
        a_s = rows_of_words(shared_in)
        chunk = a_e.shape[0] // 16
        vmem = pl.BlockSpec(memory_space=pltpu.VMEM)
        hbm = pl.BlockSpec(memory_space=pltpu.HBM)
        dma = pltpu.SemaphoreType.DMA
        operands = (
            expert_ids.T, gate_fixed.T, slot_expert.reshape(1, N), hidden, a_e, expert_out[0], a_s, shared_out
        )
        return pl.pallas_call(
            functools.partial(kernel, expert_size),
            out_shape=jax.ShapeDtypeStruct((tok, D), BF),
            in_specs=[hbm] * 8,
            out_specs=vmem,
            scratch_shapes=[
                pltpu.VMEM((topk, tok), jnp.int32),
                pltpu.VMEM((topk, tok), jnp.int32),
                pltpu.VMEM((1, N), jnp.int32),
                pltpu.VMEM((2 * tok, D), BF),
                pltpu.VMEM((2, R, tok), BF),
                pltpu.VMEM((2, R, tok), BF),
                pltpu.VMEM((2, R, tok), BF),
                pltpu.VMEM((R, D // 2), BF),
                pltpu.VMEM((R, D // 2), BF),
                pltpu.VMEM((R, D // 2), BF),
                pltpu.VMEM((R, D // 2), BF),
                pltpu.VMEM((RING, chunk, LANES), BF),
                pltpu.VMEM((2, D, F), BF),
                pltpu.VMEM((F, D), BF),
                pltpu.VMEM((2, a_s.shape[0], LANES), BF),
                pltpu.VMEM((2, 2, D, S), BF),
                pltpu.VMEM((4, S, D), BF),
                pltpu.VMEM((F // TILE, R, TILE), F32),
                pltpu.VMEM((F // TILE, R, TILE), BF),
                pltpu.VMEM((F // TILE, R, TILE), BF),
                pltpu.VMEM((R, F), BF),
                pltpu.VMEM((2, 2, 2, tok, S), F32),
                pltpu.VMEM((2, 2, 2, tok, S), BF),
                pltpu.VMEM((2, 2, 2, tok, S), BF),
                pltpu.VMEM((4, tok, S), BF),
                pltpu.VMEM((2, tok, S), BF),
                pltpu.VMEM((tok, D), F32),
                dma((64,)),
                dma((64,)),
                dma((N,)),
                dma((N,)),
                dma((N,)),
                dma((N,)),
                dma((7,)),
                dma((RING,)),
            ],
            compiler_params=pltpu.CompilerParams(
                collective_id=0, has_side_effects=True, vmem_limit_bytes=46 * 2**20 + R * 28 * 2**10
            ),
        )(*(pltpu.with_memory_space_constraint(x, pltpu.HBM) for x in operands))

    in_specs = (
        P(("dp", "expert"), "tensor"),
        P(("dp", "expert"), None),
        P(("dp", "expert"), None),
        P(),
        P(("dp", "expert"), "tensor", None, None),
        P(("dp", "expert"), None, "tensor"),
        P("tensor", None, "dp"),
        P("dp", "tensor"),
    )
    out_specs = P(("dp", "expert"), "tensor")
    return jax.shard_map(
        shards, mesh=mesh, in_specs=in_specs, out_specs=out_specs, check_vma=False
    )
```

time: 117 us -> 92.1 us (0.79)
  Pallas kernels: 109 us -> 90.3 us
  local copies, waits for them, and re-layouts: 4.14 us -> 0.88 us
  other arithmetic: 2.61 us -> 0 us
    pallas_call x1, Pallas kernels: 109 us -> 90.3 us  [shards(): pl.pallas_call(functools.partial(kernel, expert_size), out_shape=jax.Shap...]
    broadcast_in_dim x3 -> x0, local copies, waits for them, and re-layouts: 1.8 us -> none  [the longest x1 1 us: slot_plan(): gate = jnp.where(hit, gate_fixed[:, k:k + 1], gate)]
    convert_element_type x2 -> x0, other arithmetic: 1.62 us -> none  [slot_plan(): return (served.astype(BF), high.astype(BF), low.astype(BF))]
    unnamed x1, local copies, waits for them, and re-layouts: 2.06 us -> 0.88 us
where the time goes in v1:
time: 92.1 us; the launch traced here: 91.2 us
  Pallas kernels  90.3 us (98%)
    pallas_call x1, Pallas kernels, shards(): pl.pallas_call(functools.partial(kernel, expert_size), out_shape=jax.Shap...  90.3 us

profile of v1, /device:TPU:1, one launch (start us, length us, event | category | flops | bytes accessed | tf_op | source)
XLA Modules:
  0.0 91.2 jit_solution(17097910803212663469)
XLA Ops:
  0.0 90.3 %shard_map.82 = bf16[128,3072]{1,0:T(8,128)(2,1)S(1)} custom-call(s32[8,128]{1,0:T(8,128)} %bitcast.17, s32[8,128]{1,0:T(8,128)} %bitcast.18, s32[1,16]{1,0:T(1,128)} %bitcast.19, bf16[128,3072]{1,0:T(8,128)(2,1)} %hid_ref.1, bf16[49152,128]{1,0:T(8,128)(2,1)} %bitcast.14, bf16[1024,3072]{1,0:T(8,128)(2,1)} %bitcast.15, bf16[12288,128]{1,0:T(8,128)(2,1)} %bitcast.16, ...), custom_call_target="tpu_custom_call" | custom-call | tf_op jit(solution)/shard_map/pallas_call | solution.py:498
  90.3 0.9 copy.12
